TPU v7x, 32 devices: a whole 2x2x4 slice. The times are simulated.
32 devices in a mesh: rep: 8 (over z, y), fsdp: 4 (over x, core).
Axes of the slice: x: 2, y: 2, z: 4, core: 2. Of those that a mesh axis runs over, the one named last changes fastest.
Arguments:
- gradients: bfloat16 [8, 4, 1024, 2048], P('rep', 'fsdp'), may hold values from -6 to 6
- momentum: float32 [8, 1024, 2048], P('rep', None, 'fsdp'), may hold values from -12 to 12
- master_weights: float32 [1024, 2048], P(None, 'fsdp'), may hold values from -0.125 to 0.125
Outputs:
- new_momentum: float32 [8, 1024, 2048], P('rep', None, 'fsdp')
- new_master: float32 [1024, 2048], P(None, 'fsdp')
- weights_full: bfloat16 [1024, 2048], replicated
All inputs are finite; a program needn't handle non-finite values.
Results may differ from a plain program's by a relative error of at most 0.012.
Values may be sent and summed in bfloat16 or wider, within the bound.
A program may use at most 128 MiB of HBM per device.

v0:
```python
import jax
import jax.numpy as jnp
from jax import lax
from jax.sharding import PartitionSpec as P

GROUP = 128
BAND = 16


momentum_decay = 0.9
step_size = 0.05


def cosine_rows():
    freq = jnp.arange(BAND, dtype=jnp.float32)[:, None]
    place = jnp.arange(GROUP, dtype=jnp.float32)[None, :]
    factor = jnp.where(freq == 0.0, jnp.sqrt(1.0 / GROUP), jnp.sqrt(2.0 / GROUP)).astype(
        jnp.float32
    )
    return factor * jnp.cos(jnp.pi * (2.0 * place + 1.0) * freq / (2.0 * GROUP))


def band_of(matrix):
    table = cosine_rows()
    blocks = matrix.reshape(matrix.shape[0] // GROUP, GROUP, matrix.shape[1] // GROUP, GROUP)
    return jnp.einsum("kr,arbc,lc->abkl", table, blocks, table, precision=lax.Precision.HIGHEST)


def spread_band(coeffs):
    table = cosine_rows()
    blocks = jnp.einsum("kr,abkl,lc->arbc", table, coeffs, table, precision=lax.Precision.HIGHEST)
    return blocks.reshape(coeffs.shape[0] * GROUP, coeffs.shape[1] * GROUP)


def local(gradients, momentum, master_weights):
    summed = lax.psum_scatter(
        gradients[0, 0].astype(jnp.float32).astype(jnp.bfloat16),
        "fsdp",
        scatter_dimension=1,
        tiled=True,
    ).astype(jnp.float32)
    moment = momentum_decay * momentum[0] + summed
    own_band = band_of(moment)
    remaining = moment - spread_band(own_band)
    mean_band = lax.psum(own_band, "rep") / lax.axis_size("rep")
    new_master = master_weights - step_size * spread_band(mean_band)
    weights_full = lax.all_gather(new_master.astype(jnp.bfloat16), "fsdp", axis=1, tiled=True)
    return (remaining[None], new_master, weights_full)


def solution(mesh):
    return jax.shard_map(
        local,
        mesh=mesh,
        in_specs=(P("rep", "fsdp", None, None), P("rep", None, "fsdp"), P(None, "fsdp")),
        out_specs=(P("rep", None, "fsdp"), P(None, "fsdp"), P()),
        check_vma=False,
    )
```

profile of v0, /device:TPU:0, one launch (start us, length us, event | category | flops | bytes accessed | tf_op | source)
XLA Modules:
  0.0 165.8 jit_solution(8107914245681863650)
XLA Ops:
  7.2 0.0 reduce-scatter.2.cloned.1.call-start
  7.2 6.4 %copy.7 = bf16[1,1,1024,2048]{2,3,1,0:T(8,128)(2,1)} copy(bf16[1,1,1024,2048]{3,2,1,0:T(8,128)(2,1)} %param.3) | data formatting | bytes 8388608 | tf_op args[0]
  13.6 0.0 reduce-scatter.2.cloned.1.call-update
  13.6 0.0 all-gather.2.cloned.1.call-start
  13.7 1.9 %copy.6 = f32[1,1024,512]{1,2,0:T(8,128)S(1)} copy(f32[1,1024,512]{2,1,0:T(8,128)} %param.4) | data formatting | bytes 4194304 | tf_op args[1]
  15.6 2.9 %copy.10 = f32[1024,512]{0,1:T(8,128)} copy(f32[1024,512]{1,0:T(8,128)} %param.5) | data formatting | bytes 4194304 | tf_op args[2]
  18.5 42.6 %reduce-scatter.2.cloned.1.call-done = bf16[1024,512]{0,1:T(8,128)(2,1)} async-done(((bf16[1024,2048]{0,1:T(8,128)(2,1)}), bf16[1024,512]{0,1:T(8,128)(2,1)}) %reduce-scatter.2.cloned.1.call-update) | async-done | bytes 1048592 | tf_op jit(solution)/shard_map/reduce_scatter | solution.py:36
  61.1 1.5 fusion.3
  62.6 0.5 copy.16
  63.1 1.8 %fusion.13 = f32[8,4,128,16]{3,0,2,1:T(8,128)S(1)} fusion(f32[8,128,4,128]{1,0,3,2:T(8,128)S(1)} %bitcast.56, f32[128]{0:T(128)S(1)} %add_multiply_fusion, f32[16]{0:T(128)S(1)} %compare_select_fusion), kind=kOutput, calls=%fused_computation.18 | convolution fusion | flops 100669440 | bytes 2359872 | tf_op jit(solution)/shard_map/kr,arbc,lc->abkl/dot_general | solution.py:26
  65.0 3.4 %fusion.1 = f32[8,4,16,16]{3,2,1,0:T(8,128)S(1)} fusion(f32[8,4,128,16]{3,0,2,1:T(8,128)S(1)} %fusion.13, f32[128]{0:T(128)S(1)} %add_multiply_fusion, f32[16]{0:T(128)S(1)} %compare_select_fusion), kind=kOutput, calls=%fused_computation.4 | convolution fusion | flops 12589056 | bytes 295488 | tf_op jit(solution)/shard_map/kr,arbc,lc->abkl/dot_general | solution.py:26
  68.4 40.2 %psum.7 = f32[8,4,16,16]{3,2,1,0:T(8,128)S(1)} all-reduce(f32[8,4,16,16]{3,2,1,0:T(8,128)S(1)} %fusion.1), channel_id=1, replica_groups=mesh['rep'=8,'fsdp'=4] {'rep'}, use_global_device_ids=true, to_apply=%region_1.2 | all-reduce | flops 8192 | bytes 65536 | tf_op jit(solution)/shard_map/psum | solution.py:45
  108.6 0.6 fusion.4
  109.2 4.8 %multiply_bitcast_fusion = f32[8,128,4,128]{3,1,2,0:T(8,128)} fusion(f32[8,4,16,128]{3,2,1,0:T(8,128)S(1)} %fusion.4, f32[128]{0:T(128)S(1)} %add_multiply_fusion, f32[16]{0:T(128)S(1)} %compare_select_fusion), kind=kOutput, calls=%fused_computation.6 | convolution fusion | flops 101193728 | bytes 2359872 | tf_op jit(solution)/shard_map/kr,abkl,lc->arbc/dot_general | solution.py:31
  114.0 2.9 %copy.9 = f32[8,128,4,128]{1,0,3,2:T(8,128)} copy(f32[8,128,4,128]{3,1,2,0:T(8,128)} %multiply_bitcast_fusion) | data formatting | bytes 4194304 | tf_op jit(solution)/shard_map/mul | solution.py:46
  116.9 4.7 %fusion.40 = (bf16[1024,512]{0,1:T(8,128)(2,1)}, f32[1024,512]{0,1:T(8,128)}) fusion(f32[1024,512]{0,1:T(8,128)} %copy.10, f32[64,8,8,128]{3,2,1,0:T(8,128)} %bitcast.54), kind=kLoop, calls=%fused_computation.48 | loop fusion | flops 1048576 | bytes 7340032 | tf_op jit(solution)/shard_map/convert_element_type | solution.py:47
  121.6 0.6 fusion.10
  122.2 4.8 %convolution_bitcast_fusion = f32[8,128,4,128]{3,1,2,0:T(8,128)} fusion(f32[8,4,16,128]{3,2,1,0:T(8,128)S(1)} %fusion.10, f32[128]{0:T(128)S(1)} %add_multiply_fusion, f32[16]{0:T(128)S(1)} %compare_select_fusion), kind=kOutput, calls=%fused_computation.7 | convolution fusion | flops 100669440 | bytes 2359872 | tf_op jit(solution)/shard_map/kr,abkl,lc->arbc/dot_general | solution.py:31
  127.0 3.1 %copy.8 = f32[8,128,4,128]{1,0,3,2:T(8,128)} copy(f32[8,128,4,128]{3,1,2,0:T(8,128)} %convolution_bitcast_fusion) | data formatting | bytes 4194304 | tf_op jit(solution)/shard_map/kr,abkl,lc->arbc/transpose | solution.py:31
  130.1 3.8 %fusion = f32[1,1024,512]{1,2,0:T(8,128)} fusion(f32[64,8,8,128]{3,2,1,0:T(8,128)} %bitcast.55, bf16[1024,512]{0,1:T(8,128)(2,1)S(1)} %copy-done.1, f32[1,1024,512]{1,2,0:T(8,128)S(1)} %copy.6), kind=kLoop, calls=%fused_computation.2 | loop fusion | flops 2097152 | bytes 7340032 | tf_op jit(solution)/shard_map/broadcast_in_dim | solution.py:48
  133.8 3.0 %copy.11 = f32[1,1024,512]{2,1,0:T(8,128)} copy(f32[1,1024,512]{1,2,0:T(8,128)} %fusion) | data formatting | bytes 4194304
  136.9 1.8 %copy.12 = f32[1024,512]{1,0:T(8,128)} copy(f32[1024,512]{0,1:T(8,128)S(1)} %copy-done) | data formatting | bytes 4194304
  138.7 13.9 %all-gather.2.cloned.1.call-done = bf16[1024,2048]{0,1:T(8,128)(2,1)} async-done(((bf16[1024,512]{0,1:T(8,128)(2,1)}), bf16[1024,2048]{0,1:T(8,128)(2,1)}) %all-gather.2.cloned.1.call-update) | async-done | bytes 4194320 | tf_op jit(solution)/shard_map/all_gather | solution.py:47
  152.6 6.4 %copy.13 = bf16[1024,2048]{1,0:T(8,128)(2,1)} copy(bf16[1024,2048]{0,1:T(8,128)(2,1)} %all-gather.2.cloned.1.call-done) | data formatting | bytes 8388608
  (7 shorter events, 0.0 us)
Async XLA Ops:
  7.2 53.9 %reduce-scatter.2.cloned.1.call-start = ((), (), s32[]{:S(2)}) async-start(), calls=%async_computation.1 | async-start | bytes 5242880 | tf_op jit(solution)/shard_map/reduce_scatter | solution.py:36
  13.6 139.0 %all-gather.2.cloned.1.call-start = ((), (), s32[]{:S(2)}) async-start(), calls=%async_computation.2 | async-start | bytes 5242880 | tf_op jit(solution)/shard_map/all_gather | solution.py:47
  127.0 3.1 %copy-start.1 = (bf16[1024,512]{0,1:T(8,128)(2,1)S(1)}, bf16[1024,512]{0,1:T(8,128)(2,1)}, u32[]{:S(2)}) copy-start(bf16[1024,512]{0,1:T(8,128)(2,1)} %reduce-scatter.2.cloned.1.call-done) | copy-start | bytes 3145732
  133.8 3.0 %copy-start = (f32[1024,512]{0,1:T(8,128)S(1)}, f32[1024,512]{0,1:T(8,128)}, u32[]{:S(2)}) copy-start(f32[1024,512]{0,1:T(8,128)} %get-tuple-element.7) | copy-start | bytes 6291460
Sparse Core Ops, SparseCore 0:
  13.8 47.2 reduce-scatter.1
  121.7 30.8 all-gather.1
where the time goes:
time: 166 us
  waiting for transfers between devices  56.5 us (34%)
  blocking collectives  40.2 us (24%)
  local copies, waits for them, and re-layouts  28.9 us (17%)
  matrix products  16 us (10%)
  between operations  14.1 us (8%)
  other arithmetic  10 us (6%)
    reduce_scatter x1, waiting for transfers between devices, local(): lax.psum_scatter(gradients[0, 0].astype(jnp.float32).astype(jnp.bfloat16)...  42.6 us
    psum x1, blocking collectives, local(): mean_band = lax.psum(own_band, 'rep') / lax.axis_size('rep')  40.2 us
    unnamed x11, local copies, waits for them, and re-layouts  22.9 us
    all_gather x1, waiting for transfers between devices, local(): lax.all_gather(new_master.astype(jnp.bfloat16), 'fsdp', axis=1, tiled=True)  13.9 us
    dot_general x4, matrix products, spread_band(): jnp.einsum('kr,abkl,lc->arbc', table, coeffs, table, precision=lax.Precis...  10.8 us
    dot_general x2, matrix products, band_of(): jnp.einsum('kr,arbc,lc->abkl', table, blocks, table, precision=lax.Precis...  5.25 us
    convert_element_type x1, other arithmetic, local(): new_master.astype(jnp.bfloat16)  4.72 us
    broadcast_in_dim x1, other arithmetic, local(): return (remaining[None], new_master, weights_full)  3.75 us
  transfers between devices with their start and end apart: 2, of which 2 were waited for; matrix products, arithmetic and copies ran while one was open for 13% of the time, Pallas kernels for 0%

commit v1 on v0

v1 whole, which is shorter than its diff:
```python
import functools

import jax
import jax.numpy as jnp
import numpy as np
from jax import lax
from jax.experimental import pallas as pl
from jax.experimental.pallas import tpu as pltpu
from jax.sharding import PartitionSpec as P

GROUP = 128
BAND = 16
LANES = 128
HALF = LANES // 2

momentum_decay = 0.9
step_size = 0.05

MESH = pl.DeviceIdType.MESH


def cosine_rows():
    freq = np.arange(BAND, dtype=np.float64)[:, None]
    place = np.arange(GROUP, dtype=np.float64)[None, :]
    factor = np.where(freq == 0.0, np.sqrt(1.0 / GROUP), np.sqrt(2.0 / GROUP))
    return factor * np.cos(np.pi * (2.0 * place + 1.0) * freq / (2.0 * GROUP))


def tables(width):
    rows = cosine_rows()
    blocks = width // GROUP
    spread = np.zeros((HALF, width))
    for b in range(blocks):
        spread[b * BAND : (b + 1) * BAND, b * GROUP : (b + 1) * GROUP] = rows
    return rows, np.concatenate([spread, spread], axis=0)


def split(values):
    values = jnp.asarray(values, jnp.float32)
    high = values.astype(jnp.bfloat16)
    return high, (values - high.astype(jnp.float32)).astype(jnp.bfloat16)


def high_low(both):
    high = both.astype(jnp.bfloat16).astype(jnp.float32)
    lane = lax.broadcasted_iota(jnp.int32, both.shape, 1)
    return jnp.where(lane < HALF, high, both - high).astype(jnp.bfloat16)


def batches(chunks):
    if chunks < 4:
        return [(0, chunks)]
    return [(0, chunks // 2), (chunks // 2, chunks - 1), (chunks - 1, chunks)]


def exchange(
    nr, nf, grads, momentum, master, lrows, lcols,
    moment_out, raw_out, own_out, mean_out,
    gbuf, pbuf, sbuf, rbuf, mom, mout, mas, mcast, wland, bands, means,
    g_sem, mom_sem, mas_sem, mout_sem, raw_sem, own_sem, mean_sem,
    p_send, p_recv, x_send, x_recv, c_send, c_recv, m_send, m_recv,
    w_send, w_recv, f_send, f_recv, b_send, b_recv, e_send, e_recv,
):
    r, f = lax.axis_index("rep"), lax.axis_index("fsdp")
    pairs = nf // 2
    core = lax.rem(f, 2)
    pair = f // 2
    other = 1 - core
    partner = (r, pair * 2 + other)
    rows, width = momentum.shape[1], momentum.shape[2]
    chunks = rows // GROUP
    share = rows // nr
    mine = pl.ds(pl.multiple_of(r * share, share), share)

    def columns(block):
        return pl.ds(pl.multiple_of(block * width, width), width)

    mas_first = pltpu.make_async_copy(master.at[mine], mas.at[mine], mas_sem.at[0])
    mas_first.start()
    g_copies = []
    for i in range(chunks):
        at = pl.ds(i * GROUP, GROUP)
        for s in range(pairs):
            q = lax.rem(pair + s, pairs)
            c = pltpu.make_async_copy(
                grads.at[0, 0, at, columns(q * 2 + core)], gbuf.at[i, s], g_sem.at[i, s]
            )
            c.start()
            g_copies.append(c)

    barrier = pltpu.get_barrier_semaphore()
    for s in range(1, nr):
        pl.semaphore_signal(barrier, inc=1, device_id=(lax.rem(r + s, nr), f), device_id_type=MESH)
    for s in range(1, nf):
        pl.semaphore_signal(barrier, inc=1, device_id=(r, lax.rem(f + s, nf)), device_id_type=MESH)
    pl.semaphore_wait(barrier, nr - 1 + nf - 1)

    def remote(src, dst, send, recv, to):
        return pltpu.make_async_remote_copy(
            src_ref=src, dst_ref=dst, send_sem=send, recv_sem=recv, device_id=to, device_id_type=MESH
        )

    p_copies = []
    for i in range(chunks):
        at = pl.ds(i * GROUP, GROUP)
        for s in list(range(1, pairs)) + [0]:
            q = lax.rem(pair + s, pairs)
            c = remote(
                grads.at[0, 0, at, columns(q * 2 + other)], pbuf.at[i, s],
                p_send.at[i, s], p_recv.at[i, s], partner,
            )
            c.start()
            p_copies.append(c)

    mom_copies = []
    for i in range(chunks):
        at = pl.ds(i * GROUP, GROUP)
        c = pltpu.make_async_copy(momentum.at[0, at], mom.at[at], mom_sem.at[i])
        c.start()
        mom_copies.append(c)
    mas_all = pltpu.make_async_copy(master, mas.at[pl.ds(rows, rows)], mas_sem.at[1])
    mas_all.start()

    mas_first.wait()
    mcast[pl.ds(rows, share)] = mas[mine].astype(jnp.bfloat16)
    c_copies = []
    for s in range(1, pairs):
        q = lax.rem(pair + s, pairs)
        c = remote(
            mcast.at[pl.ds(rows, share)], wland.at[pairs - s - 1, mine],
            c_send.at[s - 1], c_recv.at[pairs - s - 1], (r, q * 2 + core),
        )
        c.start()
        c_copies.append(c)


    def g_at(i, s):
        return g_copies[i * pairs + s]

    def p_at(i, s):
        order = list(range(1, pairs)) + [0]
        return p_copies[i * pairs + order.index(s)]

    x_copies = []
    for i in range(chunks):
        for s in range(1, pairs):
            q = lax.rem(pair + s, pairs)
            g_at(i, s).wait()
            p_at(i, s).wait()
            sbuf[i, s - 1] = (
                gbuf[i, s].astype(jnp.float32) + pbuf[i, s].astype(jnp.float32)
            ).astype(jnp.bfloat16)
            c = remote(
                sbuf.at[i, s - 1], rbuf.at[i, pairs - s - 1],
                x_send.at[i, s - 1], x_recv.at[i, pairs - s - 1], (r, q * 2 + core),
            )
            c.start()
            x_copies.append((i, s, c))
        if i == chunks // 2 - 1:
            for s in range(pairs - 1):
                c_copies[pairs - 2 - s].wait_recv()
            w_copies = []
            for t in range(1, nr):
                for s in range(pairs - 1):
                    c = remote(
                        wland.at[s, mine], wland.at[s, mine],
                        w_send.at[s, t - 1], w_recv.at[s, nr - t - 1], (lax.rem(r + t, nr), f),
                    )
                    c.start()
                    w_copies.append(c)
    mas_all.wait()
    mcast[pl.ds(0, rows)] = mas[pl.ds(rows, rows)].astype(jnp.bfloat16)
    m_copy = remote(mcast.at[pl.ds(0, rows)], raw_out.at[f], m_send, m_recv, partner)
    m_copy.start()

    b_copies = []
    local = []
    for first, last in batches(chunks):
        for i in range(first, last):
            at = pl.ds(i * GROUP, GROUP)
            g_at(i, 0).wait()
            p_at(i, 0).wait()
            mom_copies[i].wait()
            total = gbuf[i, 0].astype(jnp.float32) + pbuf[i, 0].astype(jnp.float32)
            for j, s, c in x_copies:
                if j == i:
                    c.wait_recv()
            for s in range(pairs - 1):
                total = total + rbuf[i, s].astype(jnp.float32)
            moment = momentum_decay * mom[at] + total
            mout[at] = moment
            c = pltpu.make_async_copy(mout.at[at], moment_out.at[at], mout_sem.at[i])
            c.start()
            local.append(c)
            half = jnp.dot(
                lrows[...], moment, precision=lax.Precision.HIGHEST, preferred_element_type=jnp.float32
            )
            both = jnp.dot(
                half, lcols[...], precision=lax.Precision.HIGHEST, preferred_element_type=jnp.float32
            )
            bands[0, pl.ds(i * BAND, BAND)] = high_low(both)
        part = pl.ds(first * BAND, (last - first) * BAND)
        n = batches(chunks).index((first, last))
        for t in range(1, nr):
            c = remote(
                bands.at[0, part], bands.at[nr - t, part],
                b_send.at[n, t - 1], b_recv.at[n, nr - t - 1], (lax.rem(r + t, nr), f),
            )
            c.start()
            b_copies.append(c)
    c = pltpu.make_async_copy(bands.at[0], own_out, own_sem)
    c.start()
    local.append(c)

    for c in w_copies:
        c.wait_recv()
    f_copies = []
    for s in range(pairs - 1):
        q = lax.rem(pair + s + 1, pairs)
        c = remote(wland.at[s], raw_out.at[q * 2 + core], f_send.at[s], f_recv.at[s], partner)
        c.start()
        f_copies.append(c)
        c = pltpu.make_async_copy(wland.at[s], raw_out.at[q * 2 + core], raw_sem.at[s])
        c.start()
        local.append(c)

    for c in b_copies:
        c.wait_recv()
    total = bands[0].astype(jnp.float32)
    for t in range(1, nr):
        total = total + bands[t].astype(jnp.float32)
    means[0] = high_low((total + pltpu.roll(total, HALF, 1)) * (1.0 / nr))
    e_copies = []
    for t in range(1, nf):
        c = remote(
            means.at[0], mean_out.at[f], e_send.at[t - 1], e_recv.at[nf - t - 1],
            (r, lax.rem(f + t, nf)),
        )
        c.start()
        e_copies.append(c)
    c = pltpu.make_async_copy(means.at[0], mean_out.at[f], mean_sem)
    c.start()
    local.append(c)

    for c in local:
        c.wait()
    for c in c_copies + w_copies + b_copies + [c for _, _, c in x_copies]:
        c.wait_send()
    m_copy.wait()
    for c in f_copies + e_copies:
        c.wait()


def finish(nf, moment, master, raw, own, mean, thigh, tlow, left, f_ref, momentum_out, master_out, full_out):
    width = master.shape[1]
    f = f_ref[0]

    def spread(coeffs):
        half = jnp.dot(coeffs, thigh[...], preferred_element_type=jnp.float32)
        half = half + jnp.dot(coeffs, tlow[...], preferred_element_type=jnp.float32)
        high = half.astype(jnp.bfloat16)
        low = (half - high.astype(jnp.float32)).astype(jnp.bfloat16)
        return jnp.dot(
            left[...], jnp.concatenate([high, high, low], axis=0), preferred_element_type=jnp.float32
        )

    momentum_out[0] = moment[...] - spread(own[...])
    for j in range(nf):
        full_out[:, j * width : (j + 1) * width] = (
            raw[j].astype(jnp.float32) - step_size * spread(mean[j])
        ).astype(jnp.bfloat16)
    new_master = master[...] - step_size * spread(mean[f])
    master_out[...] = new_master
    full_out[:, pl.ds(pl.multiple_of(f * width, width), width)] = new_master.astype(jnp.bfloat16)


def local(nr, nf, gradients, momentum, master_weights):
    rows, width = master_weights.shape
    chunks = rows // GROUP
    pairs = nf // 2
    table, twice = tables(width)
    thigh, tlow = split(twice)
    lhigh, llow = split(table.T)
    left = jnp.concatenate([lhigh, llow, lhigh], axis=1)
    anywhere = pl.BlockSpec(memory_space=pl.ANY)
    vmem = pl.BlockSpec(memory_space=pltpu.VMEM)
    dma = pltpu.SemaphoreType.DMA
    bf16, f32 = jnp.bfloat16, jnp.float32
    nb = len(batches(chunks))
    share = rows // nr
    moment, raw, own, mean = pl.pallas_call(
        functools.partial(exchange, nr, nf),
        out_shape=(
            jax.ShapeDtypeStruct((rows, width), f32),
            jax.ShapeDtypeStruct((nf, rows, width), bf16),
            jax.ShapeDtypeStruct((chunks * BAND, LANES), bf16),
            jax.ShapeDtypeStruct((nf, chunks * BAND, LANES), bf16),
        ),
        in_specs=[anywhere, anywhere, anywhere, vmem, vmem],
        out_specs=(anywhere,) * 4,
        scratch_shapes=[
            pltpu.VMEM((chunks, pairs, GROUP, width), bf16),
            pltpu.VMEM((chunks, pairs, GROUP, width), bf16),
            pltpu.VMEM((chunks, pairs - 1, GROUP, width), bf16),
            pltpu.VMEM((chunks, pairs - 1, GROUP, width), bf16),
            pltpu.VMEM((rows, width), f32),
            pltpu.VMEM((rows, width), f32),
            pltpu.VMEM((2 * rows, width), f32),
            pltpu.VMEM((rows + share, width), bf16),
            pltpu.VMEM((pairs - 1, rows, width), bf16),
            pltpu.VMEM((nr, chunks * BAND, LANES), bf16),
            pltpu.VMEM((1, chunks * BAND, LANES), bf16),
            dma((chunks, pairs)),
            dma((chunks,)),
            dma((2,)),
            dma((chunks,)),
            dma((pairs - 1,)),
            dma,
            dma,
            dma((chunks, pairs)),
            dma((chunks, pairs)),
            dma((chunks, pairs - 1)),
            dma((chunks, pairs - 1)),
            dma((pairs - 1,)),
            dma((pairs - 1,)),
            dma,
            dma,
            dma((pairs - 1, nr - 1)),
            dma((pairs - 1, nr - 1)),
            dma((pairs - 1,)),
            dma((pairs - 1,)),
            dma((nb, nr - 1)),
            dma((nb, nr - 1)),
            dma((nf - 1,)),
            dma((nf - 1,)),
        ],
        compiler_params=pltpu.CompilerParams(
            collective_id=0, has_side_effects=True, vmem_limit_bytes=40 * 1024 * 1024
        ),
        name="exchange",
    )(gradients, momentum, master_weights, jnp.asarray(table, f32), jnp.asarray(twice.T, f32))

    def whole(shape):
        return pl.BlockSpec(shape, lambda a: (0,) * len(shape))

    return pl.pallas_call(
        functools.partial(finish, nf),
        grid=(chunks,),
        out_shape=(
            jax.ShapeDtypeStruct((1, rows, width), f32),
            jax.ShapeDtypeStruct((rows, width), f32),
            jax.ShapeDtypeStruct((rows, nf * width), bf16),
        ),
        in_specs=[
            pl.BlockSpec((GROUP, width), lambda a: (a, 0)),
            pl.BlockSpec((GROUP, width), lambda a: (a, 0)),
            pl.BlockSpec((nf, GROUP, width), lambda a: (0, a, 0)),
            pl.BlockSpec((BAND, LANES), lambda a: (a, 0)),
            pl.BlockSpec((nf, BAND, LANES), lambda a: (0, a, 0)),
            whole((LANES, width)),
            whole((LANES, width)),
            whole((GROUP, 3 * BAND)),
            pl.BlockSpec(memory_space=pltpu.SMEM),
        ],
        out_specs=(
            pl.BlockSpec((1, GROUP, width), lambda a: (0, a, 0)),
            pl.BlockSpec((GROUP, width), lambda a: (a, 0)),
            pl.BlockSpec((GROUP, nf * width), lambda a: (a, 0)),
        ),
        name="finish",
    )(moment, master_weights, raw, own, mean, thigh, tlow, left, lax.axis_index("fsdp").astype(jnp.int32)[None])


def solution(mesh):
    return jax.shard_map(
        functools.partial(local, mesh.shape["rep"], mesh.shape["fsdp"]),
        mesh=mesh,
        in_specs=(P("rep", "fsdp", None, None), P("rep", None, "fsdp"), P(None, "fsdp")),
        out_specs=(P("rep", None, "fsdp"), P(None, "fsdp"), P()),
        check_vma=False,
    )
```

time: 166 us -> 68.2 us (0.41)
  Pallas kernels: 0 us -> 57.7 us
  waiting for transfers between devices: 56.5 us -> 0 us
  blocking collectives: 40.2 us -> 0 us
  local copies, waits for them, and re-layouts: 28.9 us -> 9.34 us
  matrix products: 16 us -> 0 us
  between operations: 14.1 us -> 0.67 us
  other arithmetic: 10 us -> 0 us
    pallas_call x0 -> x2, Pallas kernels: none -> 57.7 us  [the longest x1 44.5 us: local(): pl.pallas_call(functools.partial(exchange, nr, nf), out_shape=(jax.ShapeD...]
    reduce_scatter x1 -> x0, waiting for transfers between devices: 42.6 us -> none  [local(): lax.psum_scatter(gradients[0, 0].astype(jnp.float32).astype(jnp.bfloat16)...]
    psum x1 -> x0, blocking collectives: 40.2 us -> none  [local(): mean_band = lax.psum(own_band, 'rep') / lax.axis_size('rep')]
    dot_general x6 -> x0, matrix products: 16 us -> none  [the longest x4 10.8 us: spread_band(): jnp.einsum('kr,abkl,lc->arbc', table, coeffs, table, precision=lax.Precis...]
    all_gather x1 -> x0, waiting for transfers between devices: 13.9 us -> none  [local(): lax.all_gather(new_master.astype(jnp.bfloat16), 'fsdp', axis=1, tiled=True)]
    unnamed x11 -> x16, local copies, waits for them, and re-layouts: 22.9 us -> 9.34 us
    convert_element_type x1 -> x0, other arithmetic: 4.72 us -> none  [local(): new_master.astype(jnp.bfloat16)]
    broadcast_in_dim x1 -> x0, other arithmetic: 3.75 us -> none  [local(): return (remaining[None], new_master, weights_full)]
  transfers between devices with their start and end apart: 2 -> 0, of which waited for: 2 -> 0; matrix products, arithmetic and copies ran while one was open for 13% -> 0% of each run, Pallas kernels for 0% -> 0%
where the time goes in v1:
time: 68.2 us; the launch traced here: 67.7 us
  Pallas kernels  57.7 us (85%)
  local copies, waits for them, and re-layouts  9.34 us (14%)
    pallas_call x1, Pallas kernels, local(): pl.pallas_call(functools.partial(exchange, nr, nf), out_shape=(jax.ShapeD...  44.5 us
    pallas_call x1, Pallas kernels, local(): pl.pallas_call(functools.partial(finish, nf), grid=(chunks,), out_shape=(...  13.2 us
    unnamed x16, local copies, waits for them, and re-layouts  9.34 us

profile of v1, /device:TPU:0, one launch (start us, length us, event | category | flops | bytes accessed | tf_op | source)
XLA Modules:
  0.0 67.7 jit_solution(12719723020954210424)
XLA Ops:
  0.6 0.0 copy-start
  0.6 1.6 %copy-done = f32[1024,512]{1,0:T(8,128)S(1)} copy-done((f32[1024,512]{1,0:T(8,128)S(1)}, f32[1024,512]{1,0:T(8,128)}, u32[]{:S(2)}) %copy-start) | copy-done | bytes 2097176
  2.2 0.0 copy-start.2
  2.2 1.6 %copy-done.2 = f32[1,1024,512]{2,1,0:T(8,128)S(1)} copy-done((f32[1,1024,512]{2,1,0:T(8,128)S(1)}, f32[1,1024,512]{2,1,0:T(8,128)}, u32[]{:S(2)}) %copy-start.2) | copy-done | bytes 2097176
  3.8 0.0 copy-start.4
  3.8 0.9 %copy-done.4 = f32[512,128]{1,0:T(8,128)S(1)} copy-done((f32[512,128]{1,0:T(8,128)S(1)}, f32[512,128]{1,0:T(8,128)}, u32[]{:S(2)}) %copy-start.4) | copy-done | bytes 262168
  4.8 0.0 copy-start.7
  4.8 0.7 %copy-done.7 = f32[16,128]{1,0:T(8,128)S(1)} copy-done((f32[16,128]{1,0:T(8,128)S(1)}, f32[16,128]{1,0:T(8,128)}, u32[]{:S(2)}) %copy-start.7) | copy-done | bytes 8216
  5.5 44.5 %exchange.1 = (f32[1024,512]{1,0:T(8,128)S(1)}, bf16[4,1024,512]{2,1,0:T(8,128)(2,1)S(1)}, bf16[128,128]{1,0:T(8,128)(2,1)S(1)}, bf16[4,128,128]{2,1,0:T(8,128)(2,1)S(1)}) custom-call(bf16[1,1,1024,2048]{3,2,1,0:T(8,128)(2,1)} %grads.1, f32[1,1024,512]{2,1,0:T(8,128)S(1)} %copy-done.2, f32[1024,512]{1,0:T(8,128)S(1)} %copy-done, f32[16,128]{1,0:T(8,128)S(1)} %copy-done.7, ...), custom_call_target="tpu_custom_call" | custom-call | tf_op jit(solution)/shard_map/exchange/pallas_call | solution.py:291
  50.0 0.0 copy-start.1
  50.0 1.9 %copy-done.1 = bf16[4,1024,512]{2,1,0:T(8,128)(2,1)} copy-done((bf16[4,1024,512]{2,1,0:T(8,128)(2,1)}, bf16[4,1024,512]{2,1,0:T(8,128)(2,1)S(1)}, u32[]{:S(2)}) %copy-start.1) | copy-done | bytes 4194328
  51.9 0.0 copy-start.3
  51.9 1.3 %copy-done.3 = f32[1024,512]{1,0:T(8,128)} copy-done((f32[1024,512]{1,0:T(8,128)}, f32[1024,512]{1,0:T(8,128)S(1)}, u32[]{:S(2)}) %copy-start.3) | copy-done | bytes 2097176
  53.2 0.0 copy-start.5
  53.2 0.7 copy-done.5
  53.9 0.0 copy-start.6
  53.9 0.6 copy-done.6
  54.5 13.2 %finish.1 = (f32[1,1024,512]{2,1,0:T(8,128)}, f32[1024,512]{1,0:T(8,128)}, bf16[1024,2048]{1,0:T(8,128)(2,1)}) custom-call(f32[1024,512]{1,0:T(8,128)} %copy-done.3, f32[1024,512]{1,0:T(8,128)} %master.3, bf16[4,1024,512]{2,1,0:T(8,128)(2,1)} %copy-done.1, bf16[128,128]{1,0:T(8,128)(2,1)} %copy-done.6, bf16[4,128,128]{2,1,0:T(8,128)(2,1)} %copy-done.5, ...), custom_call_target="tpu_custom_call" | custom-call | tf_op jit(solution)/shard_map/finish/pallas_call | solution.py:346
Async XLA Ops:
  0.6 1.6 %copy-start = (f32[1024,512]{1,0:T(8,128)S(1)}, f32[1024,512]{1,0:T(8,128)}, u32[]{:S(2)}) copy-start(f32[1024,512]{1,0:T(8,128)} %master.3) | copy-start | bytes 6291460
  2.2 1.6 %copy-start.2 = (f32[1,1024,512]{2,1,0:T(8,128)S(1)}, f32[1,1024,512]{2,1,0:T(8,128)}, u32[]{:S(2)}) copy-start(f32[1,1024,512]{2,1,0:T(8,128)} %momentum.1) | copy-start | bytes 6291460
  3.8 0.9 %copy-start.4 = (f32[512,128]{1,0:T(8,128)S(1)}, f32[512,128]{1,0:T(8,128)}, u32[]{:S(2)}) copy-start(f32[512,128]{1,0:T(8,128)} %constant.15.clone.lcols) | copy-start | bytes 786436
  4.8 0.7 %copy-start.7 = (f32[16,128]{1,0:T(8,128)S(1)}, f32[16,128]{1,0:T(8,128)}, u32[]{:S(2)}) copy-start(f32[16,128]{1,0:T(8,128)} %constant.14.clone.lrows) | copy-start | bytes 24580
  50.0 1.9 %copy-start.1 = (bf16[4,1024,512]{2,1,0:T(8,128)(2,1)}, bf16[4,1024,512]{2,1,0:T(8,128)(2,1)S(1)}, u32[]{:S(2)}) copy-start(bf16[4,1024,512]{2,1,0:T(8,128)(2,1)S(1)} %get-tuple-element.8.raw) | copy-start | bytes 12582916
  51.9 1.3 %copy-start.3 = (f32[1024,512]{1,0:T(8,128)}, f32[1024,512]{1,0:T(8,128)S(1)}, u32[]{:S(2)}) copy-start(f32[1024,512]{1,0:T(8,128)S(1)} %get-tuple-element.7.moment) | copy-start | bytes 6291460
  53.2 0.7 copy-start.5
  53.9 0.6 copy-start.6

commit v2 on v1

--- a/solution.py
+++ b/solution.py
@@ -47,6 +47,11 @@
     return jnp.where(lane < HALF, high, both - high).astype(jnp.bfloat16)
 
 
+def spread_half(coeffs, thigh, tlow):
+    half = jnp.dot(coeffs, thigh[...], preferred_element_type=jnp.float32)
+    return half + jnp.dot(coeffs, tlow[...], preferred_element_type=jnp.float32)
+
+
 def batches(chunks):
     if chunks < 4:
         return [(0, chunks)]
@@ -54,13 +59,18 @@
 
 
 def exchange(
-    nr, nf, grads, momentum, master, lrows, lcols,
-    moment_out, raw_out, own_out, mean_out,
+    nr, nf, grads, momentum, master, *rest
+):
+    hbm_tables, rest = rest[:6], rest[6:]
+    (
+    moment_out, raw_out, mean_out,
     gbuf, pbuf, sbuf, rbuf, mom, mout, mas, mcast, wland, bands, means,
-    g_sem, mom_sem, mas_sem, mout_sem, raw_sem, own_sem, mean_sem,
+    g_sem, mom_sem, mas_sem, mout_sem, raw_sem, mean_sem,
     p_send, p_recv, x_send, x_recv, c_send, c_recv, m_send, m_recv,
     w_send, w_recv, f_send, f_recv, b_send, b_recv, e_send, e_recv,
-):
+    t_sem, *vmem_tables,
+    ) = rest
+    lboth, chigh, clow, thigh, tlow, left = vmem_tables
     r, f = lax.axis_index("rep"), lax.axis_index("fsdp")
     pairs = nf // 2
     core = lax.rem(f, 2)
@@ -88,6 +98,12 @@
             c.start()
             g_copies.append(c)
 
+    t_copies = []
+    for n, (src, dst) in enumerate(zip(hbm_tables, vmem_tables)):
+        c = pltpu.make_async_copy(src, dst, t_sem.at[n])
+        c.start()
+        t_copies.append(c)
+
     barrier = pltpu.get_barrier_semaphore()
     for s in range(1, nr):
         pl.semaphore_signal(barrier, inc=1, device_id=(lax.rem(r + s, nr), f), device_id_type=MESH)
@@ -101,16 +117,16 @@
         )
 
     p_copies = []
-    for i in range(chunks):
+    order = [(i, s) for i in range(chunks) for s in range(1, pairs)] + [(i, 0) for i in range(chunks)]
+    for i, s in order:
         at = pl.ds(i * GROUP, GROUP)
-        for s in list(range(1, pairs)) + [0]:
-            q = lax.rem(pair + s, pairs)
-            c = remote(
-                grads.at[0, 0, at, columns(q * 2 + other)], pbuf.at[i, s],
-                p_send.at[i, s], p_recv.at[i, s], partner,
-            )
-            c.start()
-            p_copies.append(c)
+        q = lax.rem(pair + s, pairs)
+        c = remote(
+            grads.at[0, 0, at, columns(q * 2 + other)], pbuf.at[i, s],
+            p_send.at[i, s], p_recv.at[i, s], partner,
+        )
+        c.start()
+        p_copies.append(c)
 
     mom_copies = []
     for i in range(chunks):
@@ -138,8 +154,7 @@
         return g_copies[i * pairs + s]
 
     def p_at(i, s):
-        order = list(range(1, pairs)) + [0]
-        return p_copies[i * pairs + order.index(s)]
+        return p_copies[order.index((i, s))]
 
     x_copies = []
     for i in range(chunks):
@@ -173,8 +188,23 @@
     m_copy = remote(mcast.at[pl.ds(0, rows)], raw_out.at[f], m_send, m_recv, partner)
     m_copy.start()
 
+    for c in t_copies:
+        c.wait()
+
     b_copies = []
     local = []
+
+    def take_out(i):
+        at = pl.ds(i * GROUP, GROUP)
+        half = spread_half(bands[0, pl.ds(i * BAND, BAND)], thigh, tlow)
+        high, low = split(half)
+        mout[at] = mom[at] - jnp.dot(
+            left[...], jnp.concatenate([high, high, low], axis=0), preferred_element_type=jnp.float32
+        )
+        c = pltpu.make_async_copy(mout.at[at], moment_out.at[0, at], mout_sem.at[i])
+        c.start()
+        local.append(c)
+
     for first, last in batches(chunks):
         for i in range(first, last):
             at = pl.ds(i * GROUP, GROUP)
@@ -188,17 +218,19 @@
             for s in range(pairs - 1):
                 total = total + rbuf[i, s].astype(jnp.float32)
             moment = momentum_decay * mom[at] + total
-            mout[at] = moment
-            c = pltpu.make_async_copy(mout.at[at], moment_out.at[at], mout_sem.at[i])
-            c.start()
-            local.append(c)
-            half = jnp.dot(
-                lrows[...], moment, precision=lax.Precision.HIGHEST, preferred_element_type=jnp.float32
-            )
-            both = jnp.dot(
-                half, lcols[...], precision=lax.Precision.HIGHEST, preferred_element_type=jnp.float32
-            )
+            mom[at] = moment
+            high, low = split(moment)
+            first_part = jnp.dot(lboth[...], high, preferred_element_type=jnp.float32)
+            half = first_part[:BAND] + first_part[BAND:] + jnp.dot(
+                lboth[...], low, preferred_element_type=jnp.float32
+            )[:BAND]
+            high, low = split(half)
+            both = jnp.dot(high, chigh[...], preferred_element_type=jnp.float32)
+            both = both + jnp.dot(low, chigh[...], preferred_element_type=jnp.float32)
+            both = both + jnp.dot(high, clow[...], preferred_element_type=jnp.float32)
             bands[0, pl.ds(i * BAND, BAND)] = high_low(both)
+            if i < last - 1:
+                take_out(i)
         part = pl.ds(first * BAND, (last - first) * BAND)
         n = batches(chunks).index((first, last))
         for t in range(1, nr):
@@ -208,9 +240,7 @@
             )
             c.start()
             b_copies.append(c)
-    c = pltpu.make_async_copy(bands.at[0], own_out, own_sem)
-    c.start()
-    local.append(c)
+        take_out(last - 1)
 
     for c in w_copies:
         c.wait_recv()
@@ -251,27 +281,29 @@
         c.wait()
 
 
-def finish(nf, moment, master, raw, own, mean, thigh, tlow, left, f_ref, momentum_out, master_out, full_out):
+def finish(nf, taken, master, raw, mean, thigh, tlow, left, f_ref, momentum_out, master_out, full_out, vhigh, vlow):
     width = master.shape[1]
     f = f_ref[0]
-
-    def spread(coeffs):
-        half = jnp.dot(coeffs, thigh[...], preferred_element_type=jnp.float32)
-        half = half + jnp.dot(coeffs, tlow[...], preferred_element_type=jnp.float32)
-        high = half.astype(jnp.bfloat16)
-        low = (half - high.astype(jnp.float32)).astype(jnp.bfloat16)
-        return jnp.dot(
+    a = pl.program_id(0)
+
+    @pl.when(a == 0)
+    def _():
+        for j in range(nf):
+            vhigh[j], vlow[j] = split(spread_half(mean[j], thigh, tlow))
+
+    momentum_out[...] = taken[...]
+    part = pl.ds(pl.multiple_of(a * BAND, BAND), BAND)
+    mine = master[...]
+    new_master = mine
+    for j in range(nf):
+        high, low = vhigh[j, part], vlow[j, part]
+        delta = jnp.dot(
             left[...], jnp.concatenate([high, high, low], axis=0), preferred_element_type=jnp.float32
         )
-
-    momentum_out[0] = moment[...] - spread(own[...])
-    for j in range(nf):
-        full_out[:, j * width : (j + 1) * width] = (
-            raw[j].astype(jnp.float32) - step_size * spread(mean[j])
-        ).astype(jnp.bfloat16)
-    new_master = master[...] - step_size * spread(mean[f])
+        value = jnp.where(f == j, mine, raw[j].astype(jnp.float32)) - step_size * delta
+        new_master = jnp.where(f == j, value, new_master)
+        full_out[:, j * width : (j + 1) * width] = value.astype(jnp.bfloat16)
     master_out[...] = new_master
-    full_out[:, pl.ds(pl.multiple_of(f * width, width), width)] = new_master.astype(jnp.bfloat16)
 
 
 def local(nr, nf, gradients, momentum, master_weights):
@@ -282,22 +314,23 @@
     thigh, tlow = split(twice)
     lhigh, llow = split(table.T)
     left = jnp.concatenate([lhigh, llow, lhigh], axis=1)
+    lboth = jnp.concatenate(split(table), axis=0)
+    chigh, clow = split(twice.T)
+    small = (lboth, chigh, clow, thigh, tlow, left)
     anywhere = pl.BlockSpec(memory_space=pl.ANY)
-    vmem = pl.BlockSpec(memory_space=pltpu.VMEM)
     dma = pltpu.SemaphoreType.DMA
     bf16, f32 = jnp.bfloat16, jnp.float32
     nb = len(batches(chunks))
     share = rows // nr
-    moment, raw, own, mean = pl.pallas_call(
+    taken, raw, mean = pl.pallas_call(
         functools.partial(exchange, nr, nf),
         out_shape=(
-            jax.ShapeDtypeStruct((rows, width), f32),
+            jax.ShapeDtypeStruct((1, rows, width), f32),
             jax.ShapeDtypeStruct((nf, rows, width), bf16),
-            jax.ShapeDtypeStruct((chunks * BAND, LANES), bf16),
             jax.ShapeDtypeStruct((nf, chunks * BAND, LANES), bf16),
         ),
-        in_specs=[anywhere, anywhere, anywhere, vmem, vmem],
-        out_specs=(anywhere,) * 4,
+        in_specs=[anywhere] * (3 + len(small)),
+        out_specs=(anywhere,) * 3,
         scratch_shapes=[
             pltpu.VMEM((chunks, pairs, GROUP, width), bf16),
             pltpu.VMEM((chunks, pairs, GROUP, width), bf16),
@@ -316,7 +349,6 @@
             dma((chunks,)),
             dma((pairs - 1,)),
             dma,
-            dma,
             dma((chunks, pairs)),
             dma((chunks, pairs)),
             dma((chunks, pairs - 1)),
@@ -333,12 +365,14 @@
             dma((nb, nr - 1)),
             dma((nf - 1,)),
             dma((nf - 1,)),
-        ],
+            dma((len(small),)),
+        ]
+        + [pltpu.VMEM(t.shape, bf16) for t in small],
         compiler_params=pltpu.CompilerParams(
-            collective_id=0, has_side_effects=True, vmem_limit_bytes=40 * 1024 * 1024
+            collective_id=0, has_side_effects=True, vmem_limit_bytes=60 * 1024 * 1024
         ),
         name="exchange",
-    )(gradients, momentum, master_weights, jnp.asarray(table, f32), jnp.asarray(twice.T, f32))
+    )(gradients, momentum, master_weights, *small)
 
     def whole(shape):
         return pl.BlockSpec(shape, lambda a: (0,) * len(shape))
@@ -352,11 +386,10 @@
             jax.ShapeDtypeStruct((rows, nf * width), bf16),
         ),
         in_specs=[
-            pl.BlockSpec((GROUP, width), lambda a: (a, 0)),
+            pl.BlockSpec((1, GROUP, width), lambda a: (0, a, 0)),
             pl.BlockSpec((GROUP, width), lambda a: (a, 0)),
             pl.BlockSpec((nf, GROUP, width), lambda a: (0, a, 0)),
-            pl.BlockSpec((BAND, LANES), lambda a: (a, 0)),
-            pl.BlockSpec((nf, BAND, LANES), lambda a: (0, a, 0)),
+            whole((nf, chunks * BAND, LANES)),
             whole((LANES, width)),
             whole((LANES, width)),
             whole((GROUP, 3 * BAND)),
@@ -367,8 +400,10 @@
             pl.BlockSpec((GROUP, width), lambda a: (a, 0)),
             pl.BlockSpec((GROUP, nf * width), lambda a: (a, 0)),
         ),
+        scratch_shapes=[pltpu.VMEM((nf, chunks * BAND, width), bf16)] * 2,
+        compiler_params=pltpu.CompilerParams(vmem_limit_bytes=60 * 1024 * 1024),
         name="finish",
-    )(moment, master_weights, raw, own, mean, thigh, tlow, left, lax.axis_index("fsdp").astype(jnp.int32)[None])
+    )(taken, master_weights, raw, mean, thigh, tlow, left, lax.axis_index("fsdp").astype(jnp.int32)[None])
 
 
 def solution(mesh):

time: 68.2 us -> 55.3 us (0.81)
  local copies, waits for them, and re-layouts: 9.34 us -> 0 us
  Pallas kernels: 57.7 us -> 54.3 us
    unnamed x16 -> x0, local copies, waits for them, and re-layouts: 9.34 us -> none
    pallas_call x1, Pallas kernels: 13.2 us -> 10.1 us  [local(): pl.pallas_call(functools.partial(finish, nf), grid=(chunks,), out_shape=(...]
where the time goes in v2:
time: 55.3 us; the launch traced here: 55 us
  Pallas kernels  54.3 us (98%)
  between operations  0.64 us (1%)
    pallas_call x1, Pallas kernels, local(): pl.pallas_call(functools.partial(exchange, nr, nf), out_shape=(jax.ShapeD...  44.2 us
    pallas_call x1, Pallas kernels, local(): pl.pallas_call(functools.partial(finish, nf), grid=(chunks,), out_shape=(...  10.1 us

profile of v2, /device:TPU:0, one launch (start us, length us, event | category | flops | bytes accessed | tf_op | source)
XLA Modules:
  0.0 55.0 jit_solution(10323948636318942032)
XLA Ops:
  0.6 44.2 %exchange.1 = (f32[1,1024,512]{2,1,0:T(8,128)}, bf16[4,1024,512]{2,1,0:T(8,128)(2,1)}, bf16[4,128,128]{2,1,0:T(8,128)(2,1)}) custom-call(bf16[1,1,1024,2048]{3,2,1,0:T(8,128)(2,1)} %grads.1, f32[1,1024,512]{2,1,0:T(8,128)} %momentum.1, f32[1024,512]{1,0:T(8,128)} %master.3, bf16[32,128]{1,0:T(8,128)(2,1)} %constant.22.rest_0_, ...), custom_call_target="tpu_custom_call" | custom-call | tf_op jit(solution)/shard_map/exchange/pallas_call | solution.py:325
  44.8 10.1 %finish.1 = (f32[1,1024,512]{2,1,0:T(8,128)}, f32[1024,512]{1,0:T(8,128)}, bf16[1024,2048]{1,0:T(8,128)(2,1)}) custom-call(f32[1,1024,512]{2,1,0:T(8,128)} %get-tuple-element.6.taken, f32[1024,512]{1,0:T(8,128)} %master.3, bf16[4,1024,512]{2,1,0:T(8,128)(2,1)} %get-tuple-element.7.raw, bf16[4,128,128]{2,1,0:T(8,128)(2,1)} %get-tuple-element.8.mean, ...), custom_call_target="tpu_custom_call" | custom-call | tf_op jit(solution)/shard_map/finish/pallas_call | solution.py:380
